TPU v7x, 32 devices: a whole 2x2x4 slice. The times are simulated.
32 devices in a mesh: groups: 2 (over x), row: 16 (over z, y, core).
Axes of the slice: x: 2, y: 2, z: 4, core: 2. Of those that a mesh axis runs over, the one named last changes fastest.
Arguments:
- elevation: float32 [512, 8192], P(('groups', 'row')), parts along dimension 0, may hold values from -2048 to 4096
- bin_index: int32 [512, 8192], P(('groups', 'row')), parts along dimension 0, may hold values from 0 to 1023, as said below
- ranks: int32 [4], P('groups'), parts along dimension 0, may hold values from 20971 to 2076128, as said below
Outputs:
- shaded: float32 [512, 8192], P(('groups', 'row')), parts along dimension 0
There are 2 independent parts, one for each index of `groups`. A program takes and returns all parts, laid end to end along the dimension named above; each array names one. Nothing has to cross between parts.
Inputs may be any that keep to these rules, and one draw needn't show every extreme that they name: The bins have fixed edges: a cell with 0 < bin_index < 1023 has an elevation at or above 2 bin_index and below 2 bin_index + 2; bin 0 holds every elevation below 2 and bin 1024 - 1 every elevation at or above 2046. `ranks`: the first entry lies below 104857 and the second at or above 1992245.
All inputs are finite; a program needn't handle non-finite values.
Results may differ from a plain program's by a relative error of at most 0.0049.
Values sent between devices are 32-bit elements; how exact they have to be, the bound alone decides.
A program may use at most 64 MiB of HBM per device.

v0:
```python
import functools

import jax
import jax.numpy as jnp
from jax import lax
from jax.experimental import pallas as pl
from jax.experimental.pallas import tpu as pltpu
from jax.sharding import PartitionSpec as P

BINS = 1024
zfactor = 200.0
cos_zenith = 0.70710678
sin_zenith = 0.70710678
light_x = -0.70710678
light_y = 0.70710678
LANES = 128
HALO = 4
PAD = 128
SMOOTH = (1.0, 8.0, 28.0, 56.0, 70.0, 56.0, 28.0, 8.0, 1.0)
SLOPE = (-1.0, -6.0, -14.0, -14.0, 0.0, 14.0, 14.0, 6.0, 1.0)
UPPER = 32
LOWER = BINS // UPPER


def bins_of(cells):
    return jnp.floor(jnp.clip(cells * 0.5, 0.0, float(BINS - 1)))


def row_weights(weights, height, halo):
    rows = 8 if halo else height
    row = lax.broadcasted_iota(jnp.int32, (height, 4 * rows if halo else 3 * rows), 0)
    col = lax.broadcasted_iota(jnp.int32, row.shape, 1)
    source = lax.rem(col, rows)
    if halo:
        source = jnp.where(source < HALO, height + source, source - 8)
        source = jnp.where(col < 3 * rows, source, 4 * height)
    delta = source - row
    out = jnp.zeros(row.shape, jnp.float32)
    for k, weight in enumerate(weights):
        out = jnp.where(delta == k - HALO, weight, out)
    return out.astype(jnp.bfloat16)


def stacked(cells):
    first = cells.astype(jnp.bfloat16).astype(jnp.float32)
    rest = cells - first
    second = rest.astype(jnp.bfloat16).astype(jnp.float32)
    parts = [first, second, rest - second]
    if cells.shape[0] == 8:
        parts.append(jnp.zeros_like(first))
    return jnp.concatenate(parts, axis=0).astype(jnp.bfloat16)


def columns(x):
    wide = x.shape[1]
    for k in range(7):
        x = x + pltpu.roll(x, 1 if k % 2 else wide - 1, 1)
    moved = pltpu.roll(x, 1, 1)
    inside = slice(PAD, wide - PAD)
    return (x - moved)[:, inside], (x + moved)[:, inside]


def kernel(n, chunk, ranks_ref, elev_ref, out_ref, index, slope_x, slope_y, cells, upper, lower, send, recv, ranks, in_sem, rank_sem, halo_send, halo_recv, send_sem, recv_sem):
    me = lax.axis_index("row")
    height, width = elev_ref.shape
    chunks = width // chunk
    inner = pl.ds(PAD, width)

    load = pltpu.make_async_copy(elev_ref, cells.at[pl.ds(8, height), inner], in_sem)
    load.start()
    rank_load = pltpu.make_async_copy(ranks_ref, ranks, rank_sem)
    rank_load.start()

    barrier = pltpu.get_barrier_semaphore()

    def greet(k, carry):
        pl.semaphore_signal(barrier, inc=1, device_id={"row": lax.rem(me + k, n)},
                            device_id_type=pl.DeviceIdType.MESH)
        return carry

    lax.fori_loop(1, n, greet, 0)

    zeros = jnp.zeros((height + 8, PAD), jnp.float32)
    cells[:, pl.ds(0, PAD)] = zeros
    cells[:, pl.ds(PAD + width, PAD)] = zeros

    @pl.when(me == 0)
    def _():
        cells[4:8, inner] = jnp.zeros((4, width), jnp.float32)

    @pl.when(me == n - 1)
    def _():
        cells[0:4, inner] = jnp.zeros((4, width), jnp.float32)

    load.wait()

    down = pltpu.make_async_remote_copy(
        src_ref=cells.at[pl.ds(8 + height - HALO, HALO), inner], dst_ref=cells.at[pl.ds(4, HALO), inner],
        send_sem=halo_send.at[0], recv_sem=halo_recv.at[0],
        device_id={"row": lax.rem(me + 1, n)}, device_id_type=pl.DeviceIdType.MESH)
    up = pltpu.make_async_remote_copy(
        src_ref=cells.at[pl.ds(8, HALO), inner], dst_ref=cells.at[pl.ds(0, HALO), inner],
        send_sem=halo_send.at[1], recv_sem=halo_recv.at[1],
        device_id={"row": lax.rem(me + n - 1, n)}, device_id_type=pl.DeviceIdType.MESH)

    def prepare(i, carry):
        top, bottom = carry
        at = pl.multiple_of(i * chunk, chunk)
        block = cells[pl.ds(8, height), pl.ds(at + PAD, chunk)]
        bins = bins_of(block)
        index[:, pl.ds(at, chunk)] = bins.astype(jnp.int32)
        high = jnp.floor(bins * (1.0 / LOWER))
        upper[:, pl.ds(at, chunk)] = high
        lower[:, pl.ds(at, chunk)] = bins - high * LOWER
        for r in range(height // 8):
            for c in range(chunk // LANES):
                piece = block[8 * r : 8 * r + 8, c * LANES : (c + 1) * LANES]
                top, bottom = jnp.maximum(top, piece), jnp.minimum(bottom, piece)
        return top, bottom

    start = cells[8:16, PAD : PAD + LANES]
    top, bottom = lax.fori_loop(0, chunks, prepare, (start, start))

    urow = lax.broadcasted_iota(jnp.int32, (UPPER, chunk), 0)
    upper_iota = (4 * lax.rem(urow, 8) + urow // 8).astype(jnp.float32).astype(jnp.bfloat16)
    lower_iota = lax.broadcasted_iota(jnp.int32, (LOWER, chunk), 0).astype(jnp.float32).astype(jnp.bfloat16)

    def count(i, total):
        at = pl.multiple_of(i * chunk, chunk)
        for r in range(height):
            high = jnp.broadcast_to(upper[r : r + 1, pl.ds(at, chunk)], (UPPER, chunk)).astype(jnp.bfloat16)
            low = jnp.broadcast_to(lower[r : r + 1, pl.ds(at, chunk)], (LOWER, chunk)).astype(jnp.bfloat16)
            one, zero = jnp.ones((), jnp.bfloat16), jnp.zeros((), jnp.bfloat16)
            hot_u = jnp.where(high == upper_iota, one, zero)
            hot_l = jnp.where(low == lower_iota, one, zero)
            total = total + lax.dot_general(hot_u, hot_l, (((1,), (1,)), ((), ())),
                                            preferred_element_type=jnp.float32)
        return total

    total = lax.fori_loop(0, chunks, count, jnp.zeros((UPPER, LOWER), jnp.float32))
    counts = jnp.concatenate([total[8 * q : 8 * q + 8] for q in range(UPPER // 8)], axis=1)
    send[0:8, :] = counts
    send[8:9, :] = jnp.max(top, axis=0, keepdims=True)
    send[9:10, :] = jnp.max(-bottom, axis=0, keepdims=True)

    def copy_to(k):
        return pltpu.make_async_remote_copy(
            src_ref=send, dst_ref=recv.at[k], send_sem=send_sem.at[k], recv_sem=recv_sem.at[k],
            device_id={"row": lax.rem(me + k, n)}, device_id_type=pl.DeviceIdType.MESH)

    def post(k, carry):
        copy_to(k).start()
        return carry

    pl.semaphore_wait(barrier, n - 1)
    lax.fori_loop(1, n, post, 0)

    @pl.when(me < n - 1)
    def _():
        down.start()

    @pl.when(me > 0)
    def _():
        up.start()


    own_smooth, own_slope = row_weights(SMOOTH, height, False), row_weights(SLOPE, height, False)

    def own_rows(i, carry):
        at = pl.multiple_of(i * chunk, chunk)
        rise, level = columns(cells[pl.ds(8, height), pl.ds(at, chunk + 2 * PAD)])
        slope_x[:, pl.ds(at, chunk)] = jnp.dot(own_smooth, stacked(rise), preferred_element_type=jnp.float32)
        slope_y[:, pl.ds(at, chunk)] = jnp.dot(own_slope, stacked(level), preferred_element_type=jnp.float32)
        return carry

    lax.fori_loop(0, chunks, own_rows, 0, unroll=2)

    @pl.when(me > 0)
    def _():
        down.wait_recv()

    @pl.when(me < n - 1)
    def _():
        up.wait_recv()

    halo_smooth, halo_slope = row_weights(SMOOTH, height, True), row_weights(SLOPE, height, True)

    def halo_rows(i, carry):
        at = pl.multiple_of(i * chunk, chunk)
        rise, level = columns(cells[pl.ds(0, 8), pl.ds(at, chunk + 2 * PAD)])
        slope_x[:, pl.ds(at, chunk)] += jnp.dot(halo_smooth, stacked(rise), preferred_element_type=jnp.float32)
        slope_y[:, pl.ds(at, chunk)] += jnp.dot(halo_slope, stacked(level), preferred_element_type=jnp.float32)
        return carry

    lax.fori_loop(0, chunks, halo_rows, 0, unroll=True)

    def take(k, carry):
        copy_to(k).wait_recv()
        got = recv[k]
        return carry[0] + got[0:8], jnp.maximum(carry[1], got[8:10])

    counts, ends = lax.fori_loop(1, n, take, (send[0:8, :], send[8:10, :]))
    ends = jnp.max(ends, axis=1, keepdims=True)
    span = ends[0:1] + ends[1:2]
    scale = jnp.broadcast_to(zfactor / (8.0 * span) * (1.0 / 4096.0), (8, LANES))

    whole = counts.astype(jnp.int32)
    lane_in = lax.broadcasted_iota(jnp.int32, (LANES, LANES), 0)
    lane_out = lax.broadcasted_iota(jnp.int32, (LANES, LANES), 1)
    triangle = jnp.where(lane_in <= lane_out, 1.0, 0.0).astype(jnp.bfloat16)
    digits = jnp.concatenate([(whole & 255), ((whole >> 8) & 255), (whole >> 16), jnp.zeros_like(whole)],
                             axis=0).astype(jnp.float32).astype(jnp.bfloat16)
    sums = jnp.dot(digits, triangle, preferred_element_type=jnp.float32)
    within = sums[0:8] + 256.0 * sums[8:16] + 65536.0 * sums[16:24]
    before = jnp.zeros((1, 1), jnp.float32)
    rows = []
    rank_load.wait()
    first, second = ranks[0], ranks[1]
    for b in range(8):
        rows.append(before)
        before = before + within[b : b + 1, LANES - 1 : LANES]
    offsets = jnp.concatenate(rows, axis=0)
    cumulative = (within + offsets).astype(jnp.int32)
    divisor = jnp.full((8, LANES), second - first, jnp.int32).astype(jnp.float32)
    table = jnp.clip((cumulative - first).astype(jnp.float32) / divisor, 0.0, 1.0)
    table = table.astype(jnp.bfloat16).astype(jnp.float32)
    out_ref[0:8, :] = table
    out_ref[8:16, :] = scale

    @pl.when(me < n - 1)
    def _():
        down.wait_send()

    @pl.when(me > 0)
    def _():
        up.wait_send()

    def drain(k, carry):
        copy_to(k).wait_send()
        return carry

    lax.fori_loop(1, n, drain, 0)


def shade_kernel(chunk, sums_ref, index_ref, slope_x, slope_y, out_ref, result, out_sem):
    height, width = index_ref.shape
    chunks = width // chunk
    table = sums_ref[0:8, :]
    scale = sums_ref[8:16, :]
    tables = [jnp.broadcast_to(table[b : b + 1], (8, LANES)) for b in range(8)]

    def out_copy(i):
        at = pl.multiple_of(i * chunk, chunk)
        where = (slice(None), pl.ds(at, chunk))
        return pltpu.make_async_copy(result.at[where], out_ref.at[where], out_sem.at[i])

    def finish(i, carry):
        at = pl.multiple_of(i * chunk, chunk)
        for r in range(height // 8):
            for c in range(chunk // LANES):
                rows = pl.ds(8 * r, 8)
                cols = pl.ds(at + c * LANES, LANES)
                which = index_ref[rows, cols]
                group, lane = which >> 7, which & 127
                stretch = jnp.take_along_axis(tables[0], lane, axis=1)
                for b in range(1, 8):
                    stretch = jnp.where(group == b, jnp.take_along_axis(tables[b], lane, axis=1), stretch)
                gx = slope_x[rows, cols] * scale
                gy = slope_y[rows, cols] * scale
                light = (cos_zenith - sin_zenith * (light_x * gx + light_y * gy)) * lax.rsqrt(
                    1.0 + gx * gx + gy * gy)
                result[rows, cols] = stretch * (0.5 + jnp.maximum(light, 0.0))
        out_copy(i).start()
        return carry

    lax.fori_loop(0, chunks, finish, 0)

    def flush(i, carry):
        out_copy(i).wait()
        return carry

    lax.fori_loop(0, chunks, flush, 0)


def chunk_of(width):
    chunk = 1024
    while width % chunk:
        chunk //= 2
    return chunk


def solution(mesh):
    n = mesh.shape["row"]

    def body(elevation, bin_index, ranks):
        height, width = elevation.shape
        chunk = chunk_of(width)
        chunks = width // chunk
        grid = (height, width)
        room = 32 * height * width * 4
        block = pltpu.VMEM(grid, jnp.float32)
        whole = jax.ShapeDtypeStruct(grid, jnp.float32)
        anywhere = pl.BlockSpec(memory_space=pl.ANY)
        inside = pl.BlockSpec(memory_space=pltpu.VMEM)
        sums, index, slope_x, slope_y = pl.pallas_call(
            functools.partial(kernel, n, chunk),
            out_shape=[jax.ShapeDtypeStruct((16, LANES), jnp.float32), jax.ShapeDtypeStruct(grid, jnp.int32), whole, whole],
            in_specs=[anywhere, pl.BlockSpec(memory_space=pltpu.HBM)],
            out_specs=[inside] * 4,
            scratch_shapes=[
                pltpu.VMEM((height + 8, width + 2 * PAD), jnp.float32),
                block,
                block,
                pltpu.VMEM((10, LANES), jnp.float32),
                pltpu.VMEM((n, 10, LANES), jnp.float32),
                pltpu.SMEM((2,), jnp.int32),
                pltpu.SemaphoreType.DMA,
                pltpu.SemaphoreType.DMA,
                pltpu.SemaphoreType.DMA((2,)),
                pltpu.SemaphoreType.DMA((2,)),
                pltpu.SemaphoreType.DMA((n,)),
                pltpu.SemaphoreType.DMA((n,)),
            ],
            compiler_params=pltpu.CompilerParams(collective_id=0, has_side_effects=True, vmem_limit_bytes=room),
        )(ranks, elevation)
        return pl.pallas_call(
            functools.partial(shade_kernel, chunk),
            out_shape=whole,
            in_specs=[inside] * 4,
            out_specs=anywhere,
            scratch_shapes=[block, pltpu.SemaphoreType.DMA((chunks,))],
            compiler_params=pltpu.CompilerParams(vmem_limit_bytes=room),
        )(sums, index, slope_x, slope_y)

    in_specs = (P(("groups", "row"), None), P(("groups", "row"), None), P("groups"))
    return jax.shard_map(body, mesh=mesh, in_specs=in_specs, out_specs=P(("groups", "row"), None), check_vma=False)
```

profile of v0, /device:TPU:0, one launch (start us, length us, event | category | flops | bytes accessed | tf_op | source)
XLA Modules:
  0.0 17.1 jit_solution(6698733915612389399)
XLA Ops:
  0.0 0.0 copy-start
  0.0 1.0 %copy-done = f32[16,8192]{1,0:T(8,128)S(1)} copy-done((f32[16,8192]{1,0:T(8,128)S(1)}, f32[16,8192]{1,0:T(8,128)}, u32[]{:S(2)}) %copy-start) | copy-done | bytes 524312
  1.0 0.0 copy-start.1
  1.0 0.7 %copy-done.1 = s32[2]{0:T(128)S(1)} copy-done((s32[2]{0:T(128)S(1)}, s32[2]{0:T(128)}, u32[]{:S(2)}) %copy-start.1) | copy-done | bytes 32
  1.7 12.5 %shard_map.28 = (f32[16,128]{1,0:T(8,128)S(1)}, s32[16,8192]{1,0:T(8,128)S(1)}, f32[16,8192]{1,0:T(8,128)S(1)}, f32[16,8192]{1,0:T(8,128)S(1)}) custom-call(s32[2]{0:T(128)S(1)} %copy-done.1, f32[16,8192]{1,0:T(8,128)S(1)} %copy-done), custom_call_target="tpu_custom_call" | custom-call | tf_op jit(solution)/shard_map/pallas_call | solution.py:305
  14.2 2.9 %shard_map.29 = f32[16,8192]{1,0:T(8,128)} custom-call(f32[16,128]{1,0:T(8,128)S(1)} %get-tuple-element.9.sums_ref, s32[16,8192]{1,0:T(8,128)S(1)} %get-tuple-element.10.index_ref, f32[16,8192]{1,0:T(8,128)S(1)} %get-tuple-element.11.slope_x, f32[16,8192]{1,0:T(8,128)S(1)} %get-tuple-element.12.slope_y), custom_call_target="tpu_custom_call" | custom-call | tf_op jit(solution)/shard_map/pallas_call | solution.py:326
Async XLA Ops:
  0.0 1.0 %copy-start = (f32[16,8192]{1,0:T(8,128)S(1)}, f32[16,8192]{1,0:T(8,128)}, u32[]{:S(2)}) copy-start(f32[16,8192]{1,0:T(8,128)} %elev_ref.1) | copy-start | bytes 1572868
  1.0 0.7 %copy-start.1 = (s32[2]{0:T(128)S(1)}, s32[2]{0:T(128)}, u32[]{:S(2)}) copy-start(s32[2]{0:T(128)} %ranks_ref.1) | copy-start | bytes 28
where the time goes:
time: 17.2 us; the launch traced here: 17.1 us
  Pallas kernels  15.3 us (89%)
  local copies, waits for them, and re-layouts  1.7 us (10%)
    pallas_call x1, Pallas kernels, body(): pl.pallas_call(functools.partial(kernel, n, chunk), out_shape=[jax.ShapeD...  12.5 us
    pallas_call x1, Pallas kernels, body(): pl.pallas_call(functools.partial(shade_kernel, chunk), out_shape=whole, i...  2.89 us
    unnamed x4, local copies, waits for them, and re-layouts  1.7 us

commit v1 on v0

v1 whole, which is shorter than its diff:
```python
import functools

import jax
import jax.numpy as jnp
from jax import lax
from jax.experimental import pallas as pl
from jax.experimental.pallas import tpu as pltpu
from jax.sharding import PartitionSpec as P

BINS = 1024
zfactor = 200.0
cos_zenith = 0.70710678
sin_zenith = 0.70710678
light_x = -0.70710678
light_y = 0.70710678
LANES = 128
HALO = 4
PAD = 128
SMOOTH = (1.0, 8.0, 28.0, 56.0, 70.0, 56.0, 28.0, 8.0, 1.0)
SLOPE = (-1.0, -6.0, -14.0, -14.0, 0.0, 14.0, 14.0, 6.0, 1.0)
UPPER = 32
LOWER = BINS // UPPER
LEVELS = 1023.0
FIELD = 10
PIECES = 4
MESH = pl.DeviceIdType.MESH


def band(first):
    row = lax.broadcasted_iota(jnp.int32, (LANES, LANES), 0)
    col = lax.broadcasted_iota(jnp.int32, (LANES, LANES), 1)
    delta = row + first - col
    rise = jnp.zeros(row.shape, jnp.float32)
    level = jnp.zeros(row.shape, jnp.float32)
    for k in range(9):
        here = delta == k - HALO
        rise = jnp.where(here, SLOPE[k], rise)
        level = jnp.where(here, SMOOTH[k], level)
    return jnp.concatenate([rise, level], axis=1).astype(jnp.bfloat16)


def windows(parts, tiles):
    rows = []
    for t in range(tiles):
        for part in parts:
            rows.append(part[:, t * LANES : (t + 3) * LANES])
    return jnp.concatenate(rows, axis=0)


def partner(n, me, k):
    if n & (n - 1) == 0:
        return lax.bitwise_xor(me, n - k)
    return lax.rem(me + k, n)


def kernel(n, chunk, bins_hbm, elev_hbm, ranks_hbm, sums_ref, index_ref, slope_x, slope_y, bins, cells, halo, col_x, col_y,
           weights, send, recv, ranks, bins_sem, elev_sem, rank_sem, halo_send, halo_recv, send_sem, recv_sem):
    me = lax.axis_index("row")
    height, width = elev_hbm.shape
    chunks = width // chunk
    tiles = chunk // LANES
    inner = pl.ds(PAD, width)
    parts = halo_recv.shape[1]
    piece = width // parts

    def bins_load(half):
        where = (slice(None), pl.ds(pl.multiple_of(half * (width // 2), width // 2), width // 2))
        return pltpu.make_async_copy(bins_hbm.at[where], bins.at[where], bins_sem.at[half])

    elev_load = pltpu.make_async_copy(elev_hbm, cells.at[:, inner], elev_sem)
    rank_load = pltpu.make_async_copy(ranks_hbm, ranks, rank_sem)
    bins_load(0).start()
    bins_load(1).start()
    elev_load.start()
    rank_load.start()

    barrier = pltpu.get_barrier_semaphore()

    def greet(k, carry):
        pl.semaphore_signal(barrier, inc=1, device_id={"row": partner(n, me, k)}, device_id_type=MESH)
        return carry

    lax.fori_loop(1, n, greet, 0)

    for edge in (0, PAD + width):
        cells[:, pl.ds(edge, PAD)] = jnp.zeros((height, PAD), jnp.float32)
        halo[:, pl.ds(edge, PAD)] = jnp.zeros((8, PAD), jnp.float32)

    @pl.when(me == 0)
    def _():
        halo[4:8, inner] = jnp.zeros((4, width), jnp.float32)

    @pl.when(me == n - 1)
    def _():
        halo[0:4, inner] = jnp.zeros((4, width), jnp.float32)

    def halo_copy(way, p):
        rows = pl.ds(0, HALO) if way else pl.ds(height - HALO, HALO)
        cols = pl.ds(PAD + p * piece, piece)
        return pltpu.make_async_remote_copy(
            src_ref=cells.at[rows, cols], dst_ref=halo.at[pl.ds(0 if way else 4, HALO), cols],
            send_sem=halo_send.at[way, p], recv_sem=halo_recv.at[way, p],
            device_id={"row": lax.rem(me + n - 1, n) if way else lax.rem(me + 1, n)}, device_id_type=MESH)

    urow = lax.broadcasted_iota(jnp.int32, (UPPER, chunk), 0)
    upper_iota = (4 * lax.rem(urow, 8) + urow // 8).astype(jnp.float32).astype(jnp.bfloat16)
    lower_iota = lax.broadcasted_iota(jnp.int32, (LOWER, chunk), 0).astype(jnp.float32).astype(jnp.bfloat16)
    one, zero = jnp.ones((), jnp.bfloat16), jnp.zeros((), jnp.bfloat16)

    def count(i, total):
        whole = bins[:, pl.ds(pl.multiple_of(i * chunk, chunk), chunk)]
        high = (whole >> 5).astype(jnp.float32)
        low = (whole & 31).astype(jnp.float32)
        for r in range(height):
            hot_u = jnp.where(jnp.broadcast_to(high[r : r + 1], (UPPER, chunk)).astype(jnp.bfloat16) == upper_iota, one, zero)
            hot_l = jnp.where(jnp.broadcast_to(low[r : r + 1], (LOWER, chunk)).astype(jnp.bfloat16) == lower_iota, one, zero)
            total = total + lax.dot_general(hot_u, hot_l, (((1,), (1,)), ((), ())),
                                            preferred_element_type=jnp.float32)
        return total

    def half_count(half, total):
        bins_load(half).wait()
        for i in range(chunks // 2):
            total = count(half * (chunks // 2) + i, total)

        @pl.when(half == 0)
        def _():
            elev_load.wait()
            pl.semaphore_wait(barrier, n - 1)

            @pl.when(me < n - 1)
            def _():
                for p in range(parts):
                    halo_copy(0, p).start()

            @pl.when(me > 0)
            def _():
                for p in range(parts):
                    halo_copy(1, p).start()

        return total

    total = lax.fori_loop(0, 2, half_count, jnp.zeros((UPPER, LOWER), jnp.float32))
    tops, bottoms = [], []
    for c in range(width // LANES):
        for r in range(height // 8):
            block = cells[8 * r : 8 * r + 8, PAD + c * LANES : PAD + (c + 1) * LANES]
            if len(tops) < 4:
                tops.append(block)
                bottoms.append(block)
            else:
                at = (c * (height // 8) + r) % 4
                tops[at] = jnp.maximum(tops[at], block)
                bottoms[at] = jnp.minimum(bottoms[at], block)
    top = functools.reduce(jnp.maximum, tops)
    bottom = functools.reduce(jnp.minimum, bottoms)
    counts = jnp.concatenate([total[8 * q : 8 * q + 8] for q in range(UPPER // 8)], axis=1)
    send[0:8, :] = counts
    send[8:9, :] = jnp.max(top, axis=0, keepdims=True)
    send[9:10, :] = jnp.max(-bottom, axis=0, keepdims=True)

    def post(k, carry):
        pltpu.make_async_remote_copy(
            src_ref=send, dst_ref=recv.at[k], send_sem=send_sem, recv_sem=recv_sem,
            device_id={"row": partner(n, me, k)}, device_id_type=MESH).start()
        return carry

    lax.fori_loop(1, n, post, 0)

    for k in range(3):
        weights[k * LANES : (k + 1) * LANES, :] = band((k - 1) * LANES)
    middle = cells[0:1, PAD : PAD + 1]

    def split(x):
        x = x - middle
        first = x.astype(jnp.bfloat16).astype(jnp.float32)
        return first, x - first

    def own_rows(i, carry):
        at = pl.multiple_of(i * chunk, chunk)
        first, rest = split(cells[:, pl.ds(at, chunk + 2 * PAD)])
        got = jnp.dot(windows((first.astype(jnp.bfloat16), rest.astype(jnp.bfloat16)), tiles), weights[...],
                      preferred_element_type=jnp.float32)
        for t in range(tiles):
            both = got[2 * height * t : 2 * height * t + height] + got[2 * height * t + height : 2 * height * (t + 1)]
            col_x[i * tiles + t, 8 : 8 + height, :] = both[:, 0:LANES]
            col_y[i * tiles + t, 8 : 8 + height, :] = both[:, LANES : 2 * LANES]
        whole = bins[:, pl.ds(at, chunk)]
        group = whole >> 7
        third = jnp.where(group >= 6, 2, jnp.where(group >= 3, 1, 0))
        shift = FIELD * (group - 3 * third)
        index_ref[:, pl.ds(at, chunk)] = (third << 12) + (shift << 7) + (whole & (LANES - 1))
        return carry

    lax.fori_loop(0, chunks, own_rows, 0, unroll=4)

    def halo_rows(i):
        at = i * chunk
        first, rest = split(halo[:, pl.ds(at, chunk + 2 * PAD)])
        pair = jnp.concatenate([first, rest], axis=0).astype(jnp.bfloat16)
        got = jnp.dot(windows((pair,), tiles), weights[...], preferred_element_type=jnp.float32)
        for t in range(tiles):
            both = got[16 * t : 16 * t + 8] + got[16 * t + 8 : 16 * t + 16]
            for col, lanes in ((col_x, slice(0, LANES)), (col_y, slice(LANES, 2 * LANES))):
                col[i * tiles + t, 0:8, :] = both[:, lanes]
                col[i * tiles + t, 8 + height : 16 + height, :] = both[:, lanes]

    def down_rows(t):
        for r in range(height // 8):
            rows = [col_x[t, 8 * r + 4 + k : 8 * r + 12 + k, :] for k in range(9)]
            out = SMOOTH[4] * rows[4] + (rows[0] + rows[8])
            for k in range(1, 4):
                out = out + SMOOTH[k] * (rows[k] + rows[8 - k])
            slope_x[8 * r : 8 * r + 8, t * LANES : (t + 1) * LANES] = out
            rows = [col_y[t, 8 * r + 4 + k : 8 * r + 12 + k, :] if k != 4 else None for k in range(9)]
            out = 14.0 * ((rows[5] - rows[3]) + (rows[6] - rows[2])) + 6.0 * (rows[7] - rows[1]) + (rows[8] - rows[0])
            slope_y[8 * r : 8 * r + 8, t * LANES : (t + 1) * LANES] = out

    def arrive(p):
        @pl.when(me > 0)
        def _():
            halo_copy(0, p).wait_recv()

        @pl.when(me < n - 1)
        def _():
            halo_copy(1, p).wait_recv()

    arrive(0)
    each = chunks // parts
    for p in range(parts):
        if p + 1 < parts:
            arrive(p + 1)
        for i in range(p * each, (p + 1) * each):
            halo_rows(i)
        for t in range(p * each * tiles, (p + 1) * each * tiles):
            down_rows(t)

    rank_load.wait()
    everything = pltpu.make_async_copy(recv.at[pl.ds(1, n - 1)], recv.at[pl.ds(1, n - 1)], recv_sem)
    everything.wait()

    def take(k, carry):
        return carry[0] + recv[k, 0:8, :], jnp.maximum(carry[1], recv[k, 8:10, :])

    counts, ends = lax.fori_loop(1, n, take, (send[0:8, :], send[8:10, :]), unroll=n <= 16)
    sums_ref[0:8, :] = counts
    sums_ref[8:10, :] = ends
    sums_ref[10:11, :] = jnp.full((1, LANES), ranks[0], jnp.int32).astype(jnp.float32)
    sums_ref[11:12, :] = jnp.full((1, LANES), ranks[1], jnp.int32).astype(jnp.float32)

    @pl.when(me < n - 1)
    def _():
        for p in range(parts):
            halo_copy(0, p).wait_send()

    @pl.when(me > 0)
    def _():
        for p in range(parts):
            halo_copy(1, p).wait_send()

    pltpu.make_async_copy(recv.at[pl.ds(1, n - 1)], recv.at[pl.ds(1, n - 1)], send_sem).wait()


def shade_kernel(chunk, sums_ref, index_ref, slope_x, slope_y, out_ref, result, out_sem):
    height, width = index_ref.shape
    chunks = width // chunk

    counts = sums_ref[0:8, :]
    ends = jnp.max(sums_ref[8:10, :], axis=1, keepdims=True)
    span = ends[0:1] + ends[1:2]
    scale = jnp.broadcast_to(zfactor / (8.0 * span) * (1.0 / 4096.0), (8, LANES))
    whole = counts.astype(jnp.int32)
    lane_in = lax.broadcasted_iota(jnp.int32, (LANES, LANES), 0)
    lane_out = lax.broadcasted_iota(jnp.int32, (LANES, LANES), 1)
    triangle = jnp.where(lane_in <= lane_out, 1.0, 0.0).astype(jnp.bfloat16)
    digits = jnp.concatenate([(whole & 255), ((whole >> 8) & 255), (whole >> 16), jnp.zeros_like(whole)],
                             axis=0).astype(jnp.float32).astype(jnp.bfloat16)
    sums = jnp.dot(digits, triangle, preferred_element_type=jnp.float32)
    within = sums[0:8] + 256.0 * sums[8:16] + 65536.0 * sums[16:24]
    before = jnp.zeros((1, 1), jnp.float32)
    rows = []
    for b in range(8):
        rows.append(before)
        before = before + within[b : b + 1, LANES - 1 : LANES]
    cumulative = (within + jnp.concatenate(rows, axis=0)).astype(jnp.int32)
    first = jnp.broadcast_to(sums_ref[10:11, :], (8, LANES)).astype(jnp.int32)
    second = jnp.broadcast_to(sums_ref[11:12, :], (8, LANES)).astype(jnp.int32)
    table = jnp.clip((cumulative - first).astype(jnp.float32) / (second - first).astype(jnp.float32), 0.0, 1.0)
    fixed = jnp.floor(table * LEVELS + 0.5).astype(jnp.int32)
    spread = [jnp.broadcast_to(fixed[b : b + 1], (8, LANES)) for b in range(8)]
    words = [spread[0] + (spread[1] << FIELD) + (spread[2] << (2 * FIELD)),
             spread[3] + (spread[4] << FIELD) + (spread[5] << (2 * FIELD)),
             spread[6] + (spread[7] << FIELD)]

    def out_copy(i):
        at = pl.multiple_of(i * chunk, chunk)
        where = (slice(None), pl.ds(at, chunk))
        return pltpu.make_async_copy(result.at[where], out_ref.at[where], out_sem.at[i])

    def finish(i, carry):
        at = pl.multiple_of(i * chunk, chunk)
        for r in range(height // 8):
            for c in range(chunk // LANES):
                rows = pl.ds(8 * r, 8)
                cols = pl.ds(at + c * LANES, LANES)
                which = index_ref[rows, cols]
                lane = which & (LANES - 1)
                word = jnp.take_along_axis(words[0], lane, axis=1)
                word = jnp.where(which >= 4096, jnp.take_along_axis(words[1], lane, axis=1), word)
                word = jnp.where(which >= 8192, jnp.take_along_axis(words[2], lane, axis=1), word)
                stretch = ((word >> ((which >> 7) & 31)) & 1023).astype(jnp.float32)
                gx = slope_x[rows, cols] * scale
                gy = slope_y[rows, cols] * scale
                light = (cos_zenith - sin_zenith * (light_x * gx + light_y * gy)) * lax.rsqrt(
                    1.0 + gx * gx + gy * gy)
                result[rows, cols] = stretch * (0.5 / LEVELS + (1.0 / LEVELS) * jnp.maximum(light, 0.0))
        out_copy(i).start()
        return carry

    lax.fori_loop(0, chunks, finish, 0)

    def flush(i, carry):
        out_copy(i).wait()
        return carry

    lax.fori_loop(0, chunks, flush, 0)


def chunk_of(width):
    chunk = 1024
    while width % chunk:
        chunk //= 2
    return chunk


def solution(mesh):
    n = mesh.shape["row"]

    def body(elevation, bin_index, ranks):
        height, width = elevation.shape
        chunk = chunk_of(width)
        chunks = width // chunk
        grid = (height, width)
        room = 24 << 20
        block = pltpu.VMEM(grid, jnp.float32)
        whole = jax.ShapeDtypeStruct(grid, jnp.float32)
        anywhere = pl.BlockSpec(memory_space=pl.ANY)
        inside = pl.BlockSpec(memory_space=pltpu.VMEM)
        wide = width + 2 * PAD
        sums, index, slope_x, slope_y = pl.pallas_call(
            functools.partial(kernel, n, chunk),
            out_shape=[jax.ShapeDtypeStruct((16, LANES), jnp.float32), jax.ShapeDtypeStruct(grid, jnp.int32), whole, whole],
            in_specs=[anywhere] * 3,
            out_specs=[inside] * 4,
            scratch_shapes=[
                pltpu.VMEM(grid, jnp.int32),
                pltpu.VMEM((height, wide), jnp.float32),
                pltpu.VMEM((8, wide), jnp.float32),
                pltpu.VMEM((width // LANES, height + 16, LANES), jnp.float32),
                pltpu.VMEM((width // LANES, height + 16, LANES), jnp.float32),
                pltpu.VMEM((3 * LANES, 2 * LANES), jnp.bfloat16),
                pltpu.VMEM((10, LANES), jnp.float32),
                pltpu.VMEM((n, 10, LANES), jnp.float32),
                pltpu.SMEM((2,), jnp.int32),
                pltpu.SemaphoreType.DMA((2,)),
                pltpu.SemaphoreType.DMA,
                pltpu.SemaphoreType.DMA,
                pltpu.SemaphoreType.DMA((2, PIECES)),
                pltpu.SemaphoreType.DMA((2, PIECES)),
                pltpu.SemaphoreType.DMA,
                pltpu.SemaphoreType.DMA,
            ],
            compiler_params=pltpu.CompilerParams(collective_id=0, has_side_effects=True, vmem_limit_bytes=room),
        )(*[pltpu.with_memory_space_constraint(x, pltpu.HBM) for x in (bin_index, elevation, ranks)])
        return pl.pallas_call(
            functools.partial(shade_kernel, chunk),
            out_shape=whole,
            in_specs=[inside] * 4,
            out_specs=anywhere,
            scratch_shapes=[block, pltpu.SemaphoreType.DMA((chunks,))],
            compiler_params=pltpu.CompilerParams(vmem_limit_bytes=32 * height * width * 4),
        )(sums, index, slope_x, slope_y)

    in_specs = (P(("groups", "row"), None), P(("groups", "row"), None), P("groups"))
    return jax.shard_map(body, mesh=mesh, in_specs=in_specs, out_specs=P(("groups", "row"), None), check_vma=False)
```

time: 17.2 us -> 14 us (0.81)
  local copies, waits for them, and re-layouts: 1.7 us -> 0 us
  Pallas kernels: 15.3 us -> 13.8 us
    unnamed x4 -> x0, local copies, waits for them, and re-layouts: 1.7 us -> none
    pallas_call x1, Pallas kernels: 12.5 us -> 11.4 us  [body(): pl.pallas_call(functools.partial(kernel, n, chunk), out_shape=[jax.ShapeD...]
    pallas_call x1, Pallas kernels: 2.89 us -> 2.39 us  [body(): pl.pallas_call(functools.partial(shade_kernel, chunk), out_shape=whole, i...]
where the time goes in v1:
time: 14 us; the launch traced here: 13.8 us
  Pallas kernels  13.8 us (99%)
    pallas_call x1, Pallas kernels, body(): pl.pallas_call(functools.partial(kernel, n, chunk), out_shape=[jax.ShapeD...  11.4 us
    pallas_call x1, Pallas kernels, body(): pl.pallas_call(functools.partial(shade_kernel, chunk), out_shape=whole, i...  2.39 us

profile of v1, /device:TPU:0, one launch (start us, length us, event | category | flops | bytes accessed | tf_op | source)
XLA Modules:
  0.0 13.8 jit_solution(3883084473653431042)
XLA Ops:
  0.0 11.4 %shard_map.37 = (f32[16,128]{1,0:T(8,128)S(1)}, s32[16,8192]{1,0:T(8,128)S(1)}, f32[16,8192]{1,0:T(8,128)S(1)}, f32[16,8192]{1,0:T(8,128)S(1)}) custom-call(s32[16,8192]{1,0:T(8,128)} %bins_hbm.1, f32[16,8192]{1,0:T(8,128)} %elev_hbm.1, s32[2]{0:T(128)} %ranks_hbm.1), custom_call_target="tpu_custom_call" | custom-call | tf_op jit(solution)/shard_map/pallas_call | solution.py:350
  11.4 2.4 %shard_map.38 = f32[16,8192]{1,0:T(8,128)} custom-call(f32[16,128]{1,0:T(8,128)S(1)} %get-tuple-element.9.sums_ref, s32[16,8192]{1,0:T(8,128)S(1)} %get-tuple-element.10.index_ref, f32[16,8192]{1,0:T(8,128)S(1)} %get-tuple-element.11.slope_x, f32[16,8192]{1,0:T(8,128)S(1)} %get-tuple-element.12.slope_y), custom_call_target="tpu_custom_call" | custom-call | tf_op jit(solution)/shard_map/pallas_call | solution.py:375

commit v2 on v1

--- a/solution.py
+++ b/solution.py
@@ -20,8 +20,8 @@
 SLOPE = (-1.0, -6.0, -14.0, -14.0, 0.0, 14.0, 14.0, 6.0, 1.0)
 UPPER = 32
 LOWER = BINS // UPPER
-LEVELS = 1023.0
-FIELD = 10
+LEVELS = 255.0
+FIELD = 8
 PIECES = 4
 MESH = pl.DeviceIdType.MESH
 
@@ -47,14 +47,12 @@
     return jnp.concatenate(rows, axis=0)
 
 
-def partner(n, me, k):
-    if n & (n - 1) == 0:
-        return lax.bitwise_xor(me, n - k)
-    return lax.rem(me + k, n)
-
-
-def kernel(n, chunk, bins_hbm, elev_hbm, ranks_hbm, sums_ref, index_ref, slope_x, slope_y, bins, cells, halo, col_x, col_y,
-           weights, send, recv, ranks, bins_sem, elev_sem, rank_sem, halo_send, halo_recv, send_sem, recv_sem):
+def target(me, k):
+    return k - 1 + (k - 1 >= me).astype(jnp.int32)
+
+
+def kernel(n, chunk, bins_hbm, elev_hbm, ranks_hbm, sums_ref, bins, slope_x, slope_y, cells, halo, col_x, col_y,
+           weights, extremes, high, low, send, recv, ranks, bins_sem, elev_sem, rank_sem, halo_send, halo_recv, send_sem, recv_sem):
     me = lax.axis_index("row")
     height, width = elev_hbm.shape
     chunks = width // chunk
@@ -77,7 +75,7 @@
     barrier = pltpu.get_barrier_semaphore()
 
     def greet(k, carry):
-        pl.semaphore_signal(barrier, inc=1, device_id={"row": partner(n, me, k)}, device_id_type=MESH)
+        pl.semaphore_signal(barrier, inc=1, device_id={"row": target(me, k)}, device_id_type=MESH)
         return carry
 
     lax.fori_loop(1, n, greet, 0)
@@ -99,7 +97,7 @@
         cols = pl.ds(PAD + p * piece, piece)
         return pltpu.make_async_remote_copy(
             src_ref=cells.at[rows, cols], dst_ref=halo.at[pl.ds(0 if way else 4, HALO), cols],
-            send_sem=halo_send.at[way, p], recv_sem=halo_recv.at[way, p],
+            send_sem=halo_send.at[way], recv_sem=halo_recv.at[way, p],
             device_id={"row": lax.rem(me + n - 1, n) if way else lax.rem(me + 1, n)}, device_id_type=MESH)
 
     urow = lax.broadcasted_iota(jnp.int32, (UPPER, chunk), 0)
@@ -107,21 +105,39 @@
     lower_iota = lax.broadcasted_iota(jnp.int32, (LOWER, chunk), 0).astype(jnp.float32).astype(jnp.bfloat16)
     one, zero = jnp.ones((), jnp.bfloat16), jnp.zeros((), jnp.bfloat16)
 
-    def count(i, total):
-        whole = bins[:, pl.ds(pl.multiple_of(i * chunk, chunk), chunk)]
-        high = (whole >> 5).astype(jnp.float32)
-        low = (whole & 31).astype(jnp.float32)
+    def spread(ref, t, r):
+        row = jnp.concatenate([ref[t + c, pl.ds(r, 8, stride=0), :] for c in range(tiles)], axis=1)
+        return jnp.concatenate([row] * (UPPER // 8), axis=0).astype(jnp.bfloat16)
+
+    def count(half, i, total):
+        at = pl.multiple_of((half * (chunks // 2) + i) * chunk, chunk)
+        whole = bins[:, pl.ds(at, chunk)]
+        for c in range(tiles):
+            tile = whole[:, c * LANES : (c + 1) * LANES]
+            high[i * tiles + c] = (tile >> 5).astype(jnp.float32)
+            low[i * tiles + c] = (tile & 31).astype(jnp.float32)
         for r in range(height):
-            hot_u = jnp.where(jnp.broadcast_to(high[r : r + 1], (UPPER, chunk)).astype(jnp.bfloat16) == upper_iota, one, zero)
-            hot_l = jnp.where(jnp.broadcast_to(low[r : r + 1], (LOWER, chunk)).astype(jnp.bfloat16) == lower_iota, one, zero)
+            hot_u = jnp.where(spread(high, i * tiles, r) <= upper_iota, one, zero).astype(jnp.float8_e4m3fn)
+            hot_l = jnp.where(spread(low, i * tiles, r) <= lower_iota, one, zero).astype(jnp.float8_e4m3fn)
             total = total + lax.dot_general(hot_u, hot_l, (((1,), (1,)), ((), ())),
                                             preferred_element_type=jnp.float32)
         return total
 
+    def reach():
+        tops, bottoms = [None] * 4, [None] * 4
+        for c in range(width // LANES):
+            for r in range(height // 8):
+                block = cells[8 * r : 8 * r + 8, PAD + c * LANES : PAD + (c + 1) * LANES]
+                at = (c * (height // 8) + r) % 4
+                tops[at] = block if tops[at] is None else jnp.maximum(tops[at], block)
+                bottoms[at] = block if bottoms[at] is None else jnp.minimum(bottoms[at], block)
+        extremes[0:8, :] = functools.reduce(jnp.maximum, [x for x in tops if x is not None])
+        extremes[8:16, :] = functools.reduce(jnp.minimum, [x for x in bottoms if x is not None])
+
     def half_count(half, total):
         bins_load(half).wait()
         for i in range(chunks // 2):
-            total = count(half * (chunks // 2) + i, total)
+            total = count(half, i, total)
 
         @pl.when(half == 0)
         def _():
@@ -138,31 +154,21 @@
                 for p in range(parts):
                     halo_copy(1, p).start()
 
+            reach()
+
         return total
 
     total = lax.fori_loop(0, 2, half_count, jnp.zeros((UPPER, LOWER), jnp.float32))
-    tops, bottoms = [], []
-    for c in range(width // LANES):
-        for r in range(height // 8):
-            block = cells[8 * r : 8 * r + 8, PAD + c * LANES : PAD + (c + 1) * LANES]
-            if len(tops) < 4:
-                tops.append(block)
-                bottoms.append(block)
-            else:
-                at = (c * (height // 8) + r) % 4
-                tops[at] = jnp.maximum(tops[at], block)
-                bottoms[at] = jnp.minimum(bottoms[at], block)
-    top = functools.reduce(jnp.maximum, tops)
-    bottom = functools.reduce(jnp.minimum, bottoms)
     counts = jnp.concatenate([total[8 * q : 8 * q + 8] for q in range(UPPER // 8)], axis=1)
     send[0:8, :] = counts
-    send[8:9, :] = jnp.max(top, axis=0, keepdims=True)
-    send[9:10, :] = jnp.max(-bottom, axis=0, keepdims=True)
+    ends = [jnp.max(extremes[0:8, :], axis=0, keepdims=True), jnp.max(-extremes[8:16, :], axis=0, keepdims=True)]
+    top, bottom = [jnp.maximum(x, pltpu.roll(x, LANES // 2, 1)) for x in ends]
+    send[8:9, :] = jnp.where(lax.broadcasted_iota(jnp.int32, (1, LANES), 1) < LANES // 2, top, bottom)
 
     def post(k, carry):
         pltpu.make_async_remote_copy(
-            src_ref=send, dst_ref=recv.at[k], send_sem=send_sem, recv_sem=recv_sem,
-            device_id={"row": partner(n, me, k)}, device_id_type=MESH).start()
+            src_ref=send, dst_ref=recv.at[me], send_sem=send_sem, recv_sem=recv_sem,
+            device_id={"row": target(me, k)}, device_id_type=MESH).start()
         return carry
 
     lax.fori_loop(1, n, post, 0)
@@ -185,11 +191,6 @@
             both = got[2 * height * t : 2 * height * t + height] + got[2 * height * t + height : 2 * height * (t + 1)]
             col_x[i * tiles + t, 8 : 8 + height, :] = both[:, 0:LANES]
             col_y[i * tiles + t, 8 : 8 + height, :] = both[:, LANES : 2 * LANES]
-        whole = bins[:, pl.ds(at, chunk)]
-        group = whole >> 7
-        third = jnp.where(group >= 6, 2, jnp.where(group >= 3, 1, 0))
-        shift = FIELD * (group - 3 * third)
-        index_ref[:, pl.ds(at, chunk)] = (third << 12) + (shift << 7) + (whole & (LANES - 1))
         return carry
 
     lax.fori_loop(0, chunks, own_rows, 0, unroll=4)
@@ -240,23 +241,24 @@
     everything.wait()
 
     def take(k, carry):
-        return carry[0] + recv[k, 0:8, :], jnp.maximum(carry[1], recv[k, 8:10, :])
-
-    counts, ends = lax.fori_loop(1, n, take, (send[0:8, :], send[8:10, :]), unroll=n <= 16)
+        return carry[0] + recv[k, 0:8, :], jnp.maximum(carry[1], recv[k, 8:9, :])
+
+    recv[me] = send[...]
+    counts, ends = lax.fori_loop(1, n, take, (recv[0, 0:8, :], recv[0, 8:9, :]), unroll=n <= 16)
     sums_ref[0:8, :] = counts
-    sums_ref[8:10, :] = ends
+    sums_ref[8:9, :] = ends
     sums_ref[10:11, :] = jnp.full((1, LANES), ranks[0], jnp.int32).astype(jnp.float32)
     sums_ref[11:12, :] = jnp.full((1, LANES), ranks[1], jnp.int32).astype(jnp.float32)
 
+    edge = halo.at[pl.ds(0, HALO), inner]
+
     @pl.when(me < n - 1)
     def _():
-        for p in range(parts):
-            halo_copy(0, p).wait_send()
+        pltpu.make_async_copy(edge, edge, halo_send.at[0]).wait()
 
     @pl.when(me > 0)
     def _():
-        for p in range(parts):
-            halo_copy(1, p).wait_send()
+        pltpu.make_async_copy(edge, edge, halo_send.at[1]).wait()
 
     pltpu.make_async_copy(recv.at[pl.ds(1, n - 1)], recv.at[pl.ds(1, n - 1)], send_sem).wait()
 
@@ -266,36 +268,30 @@
     chunks = width // chunk
 
     counts = sums_ref[0:8, :]
-    ends = jnp.max(sums_ref[8:10, :], axis=1, keepdims=True)
-    span = ends[0:1] + ends[1:2]
+    ends = sums_ref[8:9, :]
+    span = (jnp.max(ends[:, 0 : LANES // 2], axis=1, keepdims=True)
+            + jnp.max(ends[:, LANES // 2 : LANES], axis=1, keepdims=True))
     scale = jnp.broadcast_to(zfactor / (8.0 * span) * (1.0 / 4096.0), (8, LANES))
-    whole = counts.astype(jnp.int32)
-    lane_in = lax.broadcasted_iota(jnp.int32, (LANES, LANES), 0)
-    lane_out = lax.broadcasted_iota(jnp.int32, (LANES, LANES), 1)
-    triangle = jnp.where(lane_in <= lane_out, 1.0, 0.0).astype(jnp.bfloat16)
-    digits = jnp.concatenate([(whole & 255), ((whole >> 8) & 255), (whole >> 16), jnp.zeros_like(whole)],
-                             axis=0).astype(jnp.float32).astype(jnp.bfloat16)
-    sums = jnp.dot(digits, triangle, preferred_element_type=jnp.float32)
-    within = sums[0:8] + 256.0 * sums[8:16] + 65536.0 * sums[16:24]
-    before = jnp.zeros((1, 1), jnp.float32)
-    rows = []
-    for b in range(8):
-        rows.append(before)
-        before = before + within[b : b + 1, LANES - 1 : LANES]
-    cumulative = (within + jnp.concatenate(rows, axis=0)).astype(jnp.int32)
+    tilt = (sin_zenith * light_y) * scale
+    lane = lax.broadcasted_iota(jnp.int32, (8, LANES), 1)
+    row = lax.broadcasted_iota(jnp.int32, (8, LANES), 0)
+    before = pltpu.roll(counts, LOWER, 1)
+    above = jnp.where(row == 0, 0.0, pltpu.roll(before, 1, 0))
+    before = jnp.where(lane < LOWER, above, before)
+    full = jnp.take_along_axis(before, lane | (LOWER - 1), axis=1, mode="promise_in_bounds")
+    cumulative = (full + (counts - before)).astype(jnp.int32)
     first = jnp.broadcast_to(sums_ref[10:11, :], (8, LANES)).astype(jnp.int32)
     second = jnp.broadcast_to(sums_ref[11:12, :], (8, LANES)).astype(jnp.int32)
     table = jnp.clip((cumulative - first).astype(jnp.float32) / (second - first).astype(jnp.float32), 0.0, 1.0)
     fixed = jnp.floor(table * LEVELS + 0.5).astype(jnp.int32)
     spread = [jnp.broadcast_to(fixed[b : b + 1], (8, LANES)) for b in range(8)]
-    words = [spread[0] + (spread[1] << FIELD) + (spread[2] << (2 * FIELD)),
-             spread[3] + (spread[4] << FIELD) + (spread[5] << (2 * FIELD)),
-             spread[6] + (spread[7] << FIELD)]
+    words = [spread[g] + (spread[g + 1] << FIELD) + (spread[g + 2] << (2 * FIELD)) + (spread[g + 3] << (3 * FIELD))
+             for g in (0, 4)]
 
     def out_copy(i):
         at = pl.multiple_of(i * chunk, chunk)
         where = (slice(None), pl.ds(at, chunk))
-        return pltpu.make_async_copy(result.at[where], out_ref.at[where], out_sem.at[i])
+        return pltpu.make_async_copy(result.at[where], out_ref.at[where], out_sem)
 
     def finish(i, carry):
         at = pl.multiple_of(i * chunk, chunk)
@@ -305,25 +301,19 @@
                 cols = pl.ds(at + c * LANES, LANES)
                 which = index_ref[rows, cols]
                 lane = which & (LANES - 1)
-                word = jnp.take_along_axis(words[0], lane, axis=1)
-                word = jnp.where(which >= 4096, jnp.take_along_axis(words[1], lane, axis=1), word)
-                word = jnp.where(which >= 8192, jnp.take_along_axis(words[2], lane, axis=1), word)
-                stretch = ((word >> ((which >> 7) & 31)) & 1023).astype(jnp.float32)
-                gx = slope_x[rows, cols] * scale
-                gy = slope_y[rows, cols] * scale
-                light = (cos_zenith - sin_zenith * (light_x * gx + light_y * gy)) * lax.rsqrt(
-                    1.0 + gx * gx + gy * gy)
+                words_at = [jnp.take_along_axis(w, lane, axis=1, mode="promise_in_bounds") for w in words]
+                word = jnp.where(which >= BINS // 2, words_at[1], words_at[0])
+                stretch = ((word >> ((which >> 4) & 24)) & 255).astype(jnp.float32)
+                rise, fall = slope_x[rows, cols], slope_y[rows, cols]
+                gx, gy = rise * scale, fall * scale
+                light = (cos_zenith - tilt * (fall - rise)) * lax.rsqrt(1.0 + gx * gx + gy * gy)
                 result[rows, cols] = stretch * (0.5 / LEVELS + (1.0 / LEVELS) * jnp.maximum(light, 0.0))
         out_copy(i).start()
         return carry
 
-    lax.fori_loop(0, chunks, finish, 0)
-
-    def flush(i, carry):
-        out_copy(i).wait()
-        return carry
-
-    lax.fori_loop(0, chunks, flush, 0)
+    lax.fori_loop(0, chunks, finish, 0, unroll=True)
+
+    pltpu.make_async_copy(result, out_ref, out_sem).wait()
 
 
 def chunk_of(width):
@@ -339,7 +329,6 @@
     def body(elevation, bin_index, ranks):
         height, width = elevation.shape
         chunk = chunk_of(width)
-        chunks = width // chunk
         grid = (height, width)
         room = 24 << 20
         block = pltpu.VMEM(grid, jnp.float32)
@@ -353,19 +342,21 @@
             in_specs=[anywhere] * 3,
             out_specs=[inside] * 4,
             scratch_shapes=[
-                pltpu.VMEM(grid, jnp.int32),
                 pltpu.VMEM((height, wide), jnp.float32),
                 pltpu.VMEM((8, wide), jnp.float32),
                 pltpu.VMEM((width // LANES, height + 16, LANES), jnp.float32),
                 pltpu.VMEM((width // LANES, height + 16, LANES), jnp.float32),
                 pltpu.VMEM((3 * LANES, 2 * LANES), jnp.bfloat16),
-                pltpu.VMEM((10, LANES), jnp.float32),
-                pltpu.VMEM((n, 10, LANES), jnp.float32),
+                pltpu.VMEM((16, LANES), jnp.float32),
+                pltpu.VMEM((width // LANES // 2, height, LANES), jnp.float32),
+                pltpu.VMEM((width // LANES // 2, height, LANES), jnp.float32),
+                pltpu.VMEM((9, LANES), jnp.float32),
+                pltpu.VMEM((n, 9, LANES), jnp.float32),
                 pltpu.SMEM((2,), jnp.int32),
                 pltpu.SemaphoreType.DMA((2,)),
                 pltpu.SemaphoreType.DMA,
                 pltpu.SemaphoreType.DMA,
-                pltpu.SemaphoreType.DMA((2, PIECES)),
+                pltpu.SemaphoreType.DMA((2,)),
                 pltpu.SemaphoreType.DMA((2, PIECES)),
                 pltpu.SemaphoreType.DMA,
                 pltpu.SemaphoreType.DMA,
@@ -377,7 +368,7 @@
             out_shape=whole,
             in_specs=[inside] * 4,
             out_specs=anywhere,
-            scratch_shapes=[block, pltpu.SemaphoreType.DMA((chunks,))],
+            scratch_shapes=[block, pltpu.SemaphoreType.DMA],
             compiler_params=pltpu.CompilerParams(vmem_limit_bytes=32 * height * width * 4),
         )(sums, index, slope_x, slope_y)
 

time: 14 us -> 12.7 us (0.907)
  Pallas kernels: 13.8 us -> 12.6 us
    pallas_call x1, Pallas kernels: 2.39 us -> 1.5 us  [body(): pl.pallas_call(functools.partial(shade_kernel, chunk), out_shape=whole, i...]
    pallas_call x1, Pallas kernels: 11.4 us -> 11.1 us  [body(): pl.pallas_call(functools.partial(kernel, n, chunk), out_shape=[jax.ShapeD...]
where the time goes in v2:
time: 12.7 us; the launch traced here: 12.6 us
  Pallas kernels  12.6 us (99%)
    pallas_call x1, Pallas kernels, body(): pl.pallas_call(functools.partial(kernel, n, chunk), out_shape=[jax.ShapeD...  11.1 us
    pallas_call x1, Pallas kernels, body(): pl.pallas_call(functools.partial(shade_kernel, chunk), out_shape=whole, i...  1.5 us

profile of v2, /device:TPU:0, one launch (start us, length us, event | category | flops | bytes accessed | tf_op | source)
XLA Modules:
  0.0 12.6 jit_solution(560204524850081375)
XLA Ops:
  0.0 11.1 %shard_map.37 = (f32[16,128]{1,0:T(8,128)S(1)}, s32[16,8192]{1,0:T(8,128)S(1)}, f32[16,8192]{1,0:T(8,128)S(1)}, f32[16,8192]{1,0:T(8,128)S(1)}) custom-call(s32[16,8192]{1,0:T(8,128)} %bins_hbm.1, f32[16,8192]{1,0:T(8,128)} %elev_hbm.1, s32[2]{0:T(128)} %ranks_hbm.1), custom_call_target="tpu_custom_call" | custom-call | tf_op jit(solution)/shard_map/pallas_call | solution.py:339
  11.1 1.5 %shard_map.38 = f32[16,8192]{1,0:T(8,128)} custom-call(f32[16,128]{1,0:T(8,128)S(1)} %get-tuple-element.9.sums_ref, s32[16,8192]{1,0:T(8,128)S(1)} %get-tuple-element.10.index_ref, f32[16,8192]{1,0:T(8,128)S(1)} %get-tuple-element.11.slope_x, f32[16,8192]{1,0:T(8,128)S(1)} %get-tuple-element.12.slope_y), custom_call_target="tpu_custom_call" | custom-call | tf_op jit(solution)/shard_map/pallas_call | solution.py:366

commit v3 on v2

--- a/solution.py
+++ b/solution.py
@@ -22,7 +22,7 @@
 LOWER = BINS // UPPER
 LEVELS = 255.0
 FIELD = 8
-PIECES = 4
+PIECES = 2
 MESH = pl.DeviceIdType.MESH
 
 
@@ -37,6 +37,12 @@
         rise = jnp.where(here, SLOPE[k], rise)
         level = jnp.where(here, SMOOTH[k], level)
     return jnp.concatenate([rise, level], axis=1).astype(jnp.bfloat16)
+
+
+def pick(table, lane):
+    numbers = lax.GatherDimensionNumbers(offset_dims=(), collapsed_slice_dims=(1,), start_index_map=(1,),
+                                         operand_batching_dims=(0,), start_indices_batching_dims=(0,))
+    return lax.gather(table, lane[..., None], numbers, slice_sizes=(1, 1), mode=lax.GatherScatterMode.PROMISE_IN_BOUNDS)
 
 
 def windows(parts, tiles):
@@ -237,30 +243,31 @@
             down_rows(t)
 
     rank_load.wait()
-    everything = pltpu.make_async_copy(recv.at[pl.ds(1, n - 1)], recv.at[pl.ds(1, n - 1)], recv_sem)
-    everything.wait()
+    first, second = ranks[0], ranks[1]
+    sums_ref[10:11, :] = jnp.full((1, LANES), first, jnp.int32).astype(jnp.float32)
+    sums_ref[11:12, :] = LEVELS / jnp.full((1, LANES), second - first, jnp.int32).astype(jnp.float32)
+    recv[me] = send[...]
+    edge = halo.at[pl.ds(0, HALO), inner]
+
+    @pl.when(me < n - 1)
+    def _():
+        pltpu.make_async_copy(edge, edge, halo_send.at[0]).wait()
+
+    @pl.when(me > 0)
+    def _():
+        pltpu.make_async_copy(edge, edge, halo_send.at[1]).wait()
+
+    everything = recv.at[pl.ds(1, n - 1)]
+    pltpu.make_async_copy(everything, everything, send_sem).wait()
+    arrivals = pltpu.make_async_copy(everything, everything, recv_sem)
+    arrivals.wait()
 
     def take(k, carry):
         return carry[0] + recv[k, 0:8, :], jnp.maximum(carry[1], recv[k, 8:9, :])
 
-    recv[me] = send[...]
     counts, ends = lax.fori_loop(1, n, take, (recv[0, 0:8, :], recv[0, 8:9, :]), unroll=n <= 16)
     sums_ref[0:8, :] = counts
     sums_ref[8:9, :] = ends
-    sums_ref[10:11, :] = jnp.full((1, LANES), ranks[0], jnp.int32).astype(jnp.float32)
-    sums_ref[11:12, :] = jnp.full((1, LANES), ranks[1], jnp.int32).astype(jnp.float32)
-
-    edge = halo.at[pl.ds(0, HALO), inner]
-
-    @pl.when(me < n - 1)
-    def _():
-        pltpu.make_async_copy(edge, edge, halo_send.at[0]).wait()
-
-    @pl.when(me > 0)
-    def _():
-        pltpu.make_async_copy(edge, edge, halo_send.at[1]).wait()
-
-    pltpu.make_async_copy(recv.at[pl.ds(1, n - 1)], recv.at[pl.ds(1, n - 1)], send_sem).wait()
 
 
 def shade_kernel(chunk, sums_ref, index_ref, slope_x, slope_y, out_ref, result, out_sem):
@@ -278,12 +285,10 @@
     before = pltpu.roll(counts, LOWER, 1)
     above = jnp.where(row == 0, 0.0, pltpu.roll(before, 1, 0))
     before = jnp.where(lane < LOWER, above, before)
-    full = jnp.take_along_axis(before, lane | (LOWER - 1), axis=1, mode="promise_in_bounds")
-    cumulative = (full + (counts - before)).astype(jnp.int32)
-    first = jnp.broadcast_to(sums_ref[10:11, :], (8, LANES)).astype(jnp.int32)
-    second = jnp.broadcast_to(sums_ref[11:12, :], (8, LANES)).astype(jnp.int32)
-    table = jnp.clip((cumulative - first).astype(jnp.float32) / (second - first).astype(jnp.float32), 0.0, 1.0)
-    fixed = jnp.floor(table * LEVELS + 0.5).astype(jnp.int32)
+    full = pick(before, lane | (LOWER - 1))
+    first = jnp.broadcast_to(sums_ref[10:11, :], (8, LANES))
+    steps = jnp.broadcast_to(sums_ref[11:12, :], (8, LANES))
+    fixed = jnp.floor(jnp.clip(((full - first) + (counts - before)) * steps, 0.0, LEVELS) + 0.5).astype(jnp.int32)
     spread = [jnp.broadcast_to(fixed[b : b + 1], (8, LANES)) for b in range(8)]
     words = [spread[g] + (spread[g + 1] << FIELD) + (spread[g + 2] << (2 * FIELD)) + (spread[g + 3] << (3 * FIELD))
              for g in (0, 4)]
@@ -301,7 +306,7 @@
                 cols = pl.ds(at + c * LANES, LANES)
                 which = index_ref[rows, cols]
                 lane = which & (LANES - 1)
-                words_at = [jnp.take_along_axis(w, lane, axis=1, mode="promise_in_bounds") for w in words]
+                words_at = [pick(w, lane) for w in words]
                 word = jnp.where(which >= BINS // 2, words_at[1], words_at[0])
                 stretch = ((word >> ((which >> 4) & 24)) & 255).astype(jnp.float32)
                 rise, fall = slope_x[rows, cols], slope_y[rows, cols]

time: 12.7 us -> 12.6 us (level)
  no operation moved by 1% of the time
where the time goes in v3:
time: 12.6 us; the launch traced here: 12.5 us
  Pallas kernels  12.5 us (99%)
    pallas_call x1, Pallas kernels, body(): pl.pallas_call(functools.partial(kernel, n, chunk), out_shape=[jax.ShapeD...  11 us
    pallas_call x1, Pallas kernels, body(): pl.pallas_call(functools.partial(shade_kernel, chunk), out_shape=whole, i...  1.49 us

profile of v3, /device:TPU:0, one launch (start us, length us, event | category | flops | bytes accessed | tf_op | source)
XLA Modules:
  0.0 12.5 jit_solution(3958115995160161176)
XLA Ops:
  0.0 11.0 %shard_map.37 = (f32[16,128]{1,0:T(8,128)S(1)}, s32[16,8192]{1,0:T(8,128)S(1)}, f32[16,8192]{1,0:T(8,128)S(1)}, f32[16,8192]{1,0:T(8,128)S(1)}) custom-call(s32[16,8192]{1,0:T(8,128)} %bins_hbm.1, f32[16,8192]{1,0:T(8,128)} %elev_hbm.1, s32[2]{0:T(128)} %ranks_hbm.1), custom_call_target="tpu_custom_call" | custom-call | tf_op jit(solution)/shard_map/pallas_call | solution.py:344
  11.0 1.5 %shard_map.38 = f32[16,8192]{1,0:T(8,128)} custom-call(f32[16,128]{1,0:T(8,128)S(1)} %get-tuple-element.9.sums_ref, s32[16,8192]{1,0:T(8,128)S(1)} %get-tuple-element.10.index_ref, f32[16,8192]{1,0:T(8,128)S(1)} %get-tuple-element.11.slope_x, f32[16,8192]{1,0:T(8,128)S(1)} %get-tuple-element.12.slope_y), custom_call_target="tpu_custom_call" | custom-call | tf_op jit(solution)/shard_map/pallas_call | solution.py:371
